TPU v7x, 32 devices: a whole 2x2x4 slice. The times are simulated.
32 devices in a mesh: tower: 8 (over y, x, core), member: 4 (over z).
Axes of the slice: x: 2, y: 2, z: 4, core: 2. Of those that a mesh axis runs over, the one named last changes fastest.
Arguments:
- slabs: bfloat16 [8, 1024, 4096], P('tower', None, 'member'), may hold values from -6 to 6
- cross_down: bfloat16 [8, 2, 4096, 512], P('tower', None, None, 'member'), may hold values from -0.09375 to 0.09375
- cross_up: bfloat16 [8, 2, 4096, 512], P('tower', None, None, 'member'), may hold values from -0.25 to 0.25
- cross_bias: float32 [8, 2, 4096], P('tower'), may hold values from -3 to 3
- projector: bfloat16 [8, 4096, 2048], P('tower'), may hold values from -0.09375 to 0.09375
- placement: int32 [8, 32], P('tower'), may hold values from 0 to 31, each once within a row
- owner: int32 [4, 256], replicated, may hold values from 0 to 255, each once within a row
- inter_grad: bfloat16 [1024, 16384], P(('tower', 'member')), may hold values from -6 to 6
Outputs:
- interactions: float32 [1024, 16384], P(('tower', 'member'))
- slab_grad: bfloat16 [8, 1024, 4096], P('tower', None, 'member')
Inputs may be any that keep to these rules, and one draw needn't show every extreme that they name: Each row of placement names every feature of its tower once. Each row of owner names every sample of its block once.
All inputs are finite; a program needn't handle non-finite values.
Results may differ from a plain program's by a relative error of at most 0.018.
Values may be sent and summed in bfloat16 or wider, within the bound.
No kernel may reach another device: no remote copies, remote signals or barrier semaphores. Data moves between devices by JAX's collectives and lax.ppermute only.
A program may use at most 128 MiB of HBM per device.

v0:
```python
import jax
import jax.numpy as jnp
from jax import lax
from jax.sharding import PartitionSpec as P


def per_device(slabs, cross_down, cross_up, cross_bias, projector, placement, owner, inter_grad):
    gathered = lax.all_to_all(slabs, "member", split_axis=1, concat_axis=2, tiled=True)
    row_count = gathered.shape[1]
    full_width = gathered.shape[2]
    features = placement.shape[1]
    slot_width = full_width // features
    depth_count = cross_down.shape[1]
    order = placement[0]
    inputs = (
        gathered[0]
        .reshape(row_count, features, slot_width)[:, order]
        .reshape(row_count, full_width)
    )
    inputs_f = inputs.astype(jnp.float32)
    biases = cross_bias[0]
    whole_down, whole_up = (
        lax.all_gather(cross_down, "member", axis=3, tiled=True),
        lax.all_gather(cross_up, "member", axis=3, tiled=True),
    )
    current = inputs
    scales = []
    for depth in range(depth_count):
        hidden = jnp.dot(current, whole_down[0, depth], preferred_element_type=jnp.float32).astype(
            jnp.bfloat16
        )
        scale_now = (
            jnp.dot(hidden, whole_up[0, depth].T, preferred_element_type=jnp.float32)
            + biases[depth]
        )
        scales.append(scale_now)
        current = (inputs_f * scale_now + current.astype(jnp.float32)).astype(jnp.bfloat16)
    vector = jnp.dot(current, projector[0], preferred_element_type=jnp.float32).astype(jnp.bfloat16)
    own_row = lax.dynamic_index_in_dim(owner, lax.axis_index("member"), 0, keepdims=False)
    ordered = vector[own_row]
    owned = lax.all_to_all(ordered[:, None, :], "tower", split_axis=0, concat_axis=1, tiled=True)
    owned_rows = owned.shape[0]
    tower_count = owned.shape[1]
    owned_f = owned.reshape(owned_rows, -1, slot_width).astype(jnp.float32)
    vector_count = owned_f.shape[1]
    table = jnp.einsum("bie,bje->bij", owned_f, owned_f) / slot_width
    interactions = table.reshape(owned_rows, vector_count * vector_count)
    cotangent = inter_grad.astype(jnp.float32).reshape(owned_rows, vector_count, vector_count)
    symmetric = cotangent + jnp.swapaxes(cotangent, 1, 2)
    vec_grad = (jnp.einsum("bij,bje->bie", symmetric, owned_f) / slot_width).astype(jnp.bfloat16)
    vec_grad = vec_grad.reshape(owned_rows, tower_count, -1)
    returned = lax.all_to_all(vec_grad, "tower", split_axis=1, concat_axis=0, tiled=True)
    inverse_own = jnp.argsort(own_row)
    local_grad = returned[:, 0, :][inverse_own]
    gradient = jnp.dot(local_grad, projector[0].T, preferred_element_type=jnp.float32)
    accum = jnp.zeros((row_count, full_width), jnp.float32)
    for depth in reversed(range(depth_count)):
        accum = accum + gradient * scales[depth]
        dscale = (gradient * inputs_f).astype(jnp.bfloat16)
        dhidden = jnp.dot(dscale, whole_up[0, depth], preferred_element_type=jnp.float32).astype(
            jnp.bfloat16
        )
        gradient = gradient + jnp.dot(
            dhidden, whole_down[0, depth].T, preferred_element_type=jnp.float32
        )
    total = (gradient + accum).astype(jnp.bfloat16)
    inverse_place = jnp.argsort(order)
    unplaced = total.reshape(row_count, features, slot_width)[:, inverse_place].reshape(
        1, row_count, full_width
    )
    slab_grad = lax.all_to_all(unplaced, "member", split_axis=2, concat_axis=1, tiled=True)
    return (interactions, slab_grad)


def solution(mesh):
    placed = (
        P("tower", None, "member"),
        P("tower", None, None, "member"),
        P("tower", None, None, "member"),
        P("tower", None, None),
        P("tower", None, None),
        P("tower", None),
        P(),
        P(("tower", "member"), None),
    )
    return jax.shard_map(
        per_device,
        mesh=mesh,
        in_specs=placed,
        out_specs=(P(("tower", "member"), None), P("tower", None, "member")),
        check_vma=False,
    )
```

profile of v0, /device:TPU:2, one launch (start us, length us, event | category | flops | bytes accessed | tf_op | source)
XLA Modules:
  0.0 606.8 jit_solution(234920576451379751)
XLA Ops:
  7.2 0.0 copy-start.2
  7.2 0.0 all-gather.3.cloned.1.call-start
  7.2 0.7 all-gather.3.cloned.1.call-update
  7.9 0.0 all-gather.5.cloned.1.call-start
  8.0 0.7 all-gather.5.cloned.1.call-update
  8.7 0.1 copy-done.2
  8.8 5.2 copy.92
  13.9 0.6 broadcast.88
  14.5 12.8 %reduce = bf16[1024,1024]{1,0:T(8,128)(2,1)S(1)} reduce(bf16[1024,1,1024]{2,1,0:T(2,128)(2,1)} %bitcast.161, bf16[]{:T(256)} %broadcast.88), dimensions={1}, to_apply=%bitcast.157.reduce_sub_computation | reduce | bytes 4194306
  27.3 0.0 copy-start.4
  27.3 0.0 copy-start.3
  27.3 2.8 reshape.136
  30.1 5.3 all-to-all-start
  35.4 0.7 compare_select_fusion
  36.1 0.0 copy-done.4
  36.2 0.0 copy-done.3
  36.2 101.2 %all-to-all-done = bf16[4,2,131072]{2,1,0:T(2,128)(2,1)S(1)} async-done(((bf16[4,2,131072]{2,1,0:T(2,128)(2,1)}), bf16[4,2,131072]{2,1,0:T(2,128)(2,1)S(1)}, u32[]{:S(2)}, u32[]{:S(2)}) %all-to-all-start) | async-done | bytes 2097184 | tf_op jit(solution)/shard_map/all_to_all | solution.py:8
  137.4 3.4 reshape.137
  140.8 3.1 copy.52
  143.9 2.6 copy.41
  146.4 4.1 copy.42
  150.5 2.5 gather_fusion
  153.1 53.1 %all-gather.3.cloned.1.call-done = bf16[1,2,4096,512]{3,2,1,0:T(8,128)(2,1)} async-done(((bf16[1,2,4096,128]{3,2,1,0:T(8,128)(2,1)}), bf16[1,2,4096,512]{3,2,1,0:T(8,128)(2,1)}) %all-gather.3.cloned.1.call-update) | async-done | bytes 8388624 | tf_op jit(solution)/shard_map/all_gather | solution.py:23
  206.2 151.8 %all-gather.5.cloned.1.call-done = bf16[1,2,4096,512]{3,2,1,0:T(8,128)(2,1)} async-done(((bf16[1,2,4096,128]{3,2,1,0:T(8,128)(2,1)}), bf16[1,2,4096,512]{3,2,1,0:T(8,128)(2,1)}) %all-gather.5.cloned.1.call-update) | async-done | bytes 8388624 | tf_op jit(solution)/shard_map/all_gather | solution.py:24
  357.9 7.8 %convolution_add_fusion.3 = f32[256,4096]{1,0:T(8,128)} fusion(bf16[1,2,4096,512]{3,2,1,0:T(8,128)(2,1)} %all-gather.5.cloned.1.call-done, f32[4096]{0:T(1024)S(1)} %bitcast.177, bf16[1,2,4096,512]{3,2,1,0:T(8,128)(2,1)} %all-gather.3.cloned.1.call-done, bf16[32,256,128]{2,1,0:T(8,128)(2,1)S(1)} %gather_fusion), kind=kOutput, calls=%fused_computation.16 | convolution fusion | flops 2148663296 | bytes 14696448 | tf_op jit(solution)/shard_map/dot_general | solution.py:33
  365.7 9.1 %convolution_add_fusion.2 = f32[256,4096]{1,0:T(8,128)} fusion(bf16[1,2,4096,512]{3,2,1,0:T(8,128)(2,1)} %all-gather.5.cloned.1.call-done, f32[4096]{0:T(1024)S(1)} %bitcast.176, bf16[1,2,4096,512]{3,2,1,0:T(8,128)(2,1)} %all-gather.3.cloned.1.call-done, f32[256,4096]{1,0:T(8,128)} %convolution_add_fusion.3, bf16[32,256,128]{2,1,0:T(8,128)(2,1)S(1)} %gather_fusion), kind=kOutput, calls=%fused_computation.15 | convolution fusion | flops 2152857600 | bytes 18890752 | tf_op jit(solution)/shard_map/dot_general | solution.py:33
  374.8 12.7 %fusion.15 = bf16[256,2048]{1,0:T(8,128)(2,1)S(1)} fusion(bf16[1,4096,2048]{2,1,0:T(8,128)(2,1)} %param.12, f32[256,4096]{1,0:T(8,128)} %convolution_add_fusion.2, f32[256,4096]{1,0:T(8,128)} %convolution_add_fusion.3, bf16[32,256,128]{2,1,0:T(8,128)(2,1)S(1)} %gather_fusion), kind=kOutput, calls=%fused_computation.32 | convolution fusion | flops 4303880192 | bytes 28311552 | tf_op jit(solution)/shard_map/dot_general | solution.py:38
  387.5 1.4 gather_fusion.1
  388.9 1.4 reduce.1
  390.3 1.8 reshape.138
  392.1 4.2 all-to-all-start.1
  396.3 1.4 convert_bitcast_fusion
  397.7 0.4 copy.58
  398.1 1.8 copy.46
  399.9 10.3 %all-to-all-done.1 = bf16[8,2,32768]{2,1,0:T(2,128)(2,1)S(1)} async-done(((bf16[8,2,32768]{2,1,0:T(2,128)(2,1)}), bf16[8,2,32768]{2,1,0:T(2,128)(2,1)S(1)}, u32[]{:S(2)}, u32[]{:S(2)}) %all-to-all-start.1) | async-done | bytes 1048608 | tf_op jit(solution)/shard_map/all_to_all | solution.py:41
  410.2 3.4 reshape.139
  413.6 2.2 copy.53
  415.8 1.5 copy.45
  417.4 1.6 reshape.92
  418.9 3.0 multiply_convert_fusion
  421.9 1.5 reshape.96
  423.5 1.5 copy.47
  425.0 5.0 all-to-all-start.2
  430.0 3.2 sort.34
  433.2 1.6 sort.35
  434.8 9.1 %all-to-all-done.2 = bf16[32,8,2048]{2,0,1:T(8,128)(2,1)S(1)} async-done(((bf16[32,8,2048]{2,0,1:T(8,128)(2,1)}), bf16[32,8,2048]{2,0,1:T(8,128)(2,1)S(1)}, u32[]{:S(2)}, u32[]{:S(2)}) %all-to-all-start.2) | async-done | bytes 1048608 | tf_op jit(solution)/shard_map/all_to_all | solution.py:52
  443.9 2.3 gather_fusion.2
  446.2 12.7 %fusion = f32[256,4096]{1,0:T(8,128)} fusion(bf16[256,2048]{1,0:T(8,128)(2,1)} %gather_fusion.2, bf16[1,4096,2048]{2,1,0:T(8,128)(2,1)} %param.12), kind=kOutput, calls=%fused_computation.4 | convolution fusion | flops 4294967296 | bytes 22020096 | tf_op jit(solution)/shard_map/dot_general | solution.py:55
  458.9 0.0 copy-done.1
  458.9 10.2 %convolution_add_fusion.1 = f32[256,4096]{1,0:T(8,128)} fusion(f32[256,4096]{1,0:T(8,128)} %fusion, bf16[1,2,4096,512]{3,2,1,0:T(8,128)(2,1)} %all-gather.3.cloned.1.call-done, bf16[1,2,4096,512]{3,2,1,0:T(8,128)(2,1)} %all-gather.5.cloned.1.call-done, bf16[32,256,128]{2,1,0:T(8,128)(2,1)S(1)} %copy-done.1), kind=kOutput, calls=%fused_computation.14 | convolution fusion | flops 2151809024 | bytes 23068672 | tf_op jit(solution)/shard_map/dot_general | solution.py:63
  469.2 13.5 %fusion.26 = bf16[32,32,8,128]{3,2,1,0:T(8,128)(2,1)} fusion(f32[256,4096]{1,0:T(8,128)} %convolution_add_fusion.1, f32[256,4096]{1,0:T(8,128)} %convolution_add_fusion.3, f32[256,4096]{1,0:T(8,128)} %fusion, f32[256,4096]{1,0:T(8,128)} %convolution_add_fusion.2, bf16[1,2,4096,512]{3,2,1,0:T(8,128)(2,1)} %all-gather.3.cloned.1.call-done, ...), kind=kOutput, calls=%fused_computation.43 | convolution fusion | flops 2157051904 | bytes 33554432 | tf_op jit(solution)/shard_map/dot_general | solution.py:63
  482.7 2.2 copy.90
  484.8 2.1 gather_fusion.3
  487.0 3.3 copy.49
  490.2 25.3 %copy.91 = bf16[1,256,4096]{1,0,2:T(2,128)(2,1)} copy(bf16[1,256,4096]{1,2,0:T(8,128)(2,1)S(1)} %bitcast.166) | data formatting | bytes 4194304 | tf_op jit(solution)/shard_map/reshape | solution.py:68
  515.5 21.6 %reduce.2 = bf16[4096,256]{1,0:T(8,128)(2,1)S(1)} reduce(bf16[4096,1,256]{2,1,0:T(2,128)(2,1)} %bitcast.162, bf16[]{:T(256)} %broadcast.88), dimensions={1}, to_apply=%bitcast.156.reduce_sub_computation | reduce | bytes 4194306
  537.1 2.1 reshape.140
  539.2 3.6 all-to-all-start.3
  542.8 0.8 convolution_multiply_fusion
  543.6 2.5 copy.89
  546.2 45.3 %all-to-all-done.3 = bf16[4,2,131072]{2,1,0:T(2,128)(2,1)S(1)} async-done(((bf16[4,2,131072]{2,1,0:T(2,128)(2,1)}), bf16[4,2,131072]{2,1,0:T(2,128)(2,1)S(1)}, u32[]{:S(2)}, u32[]{:S(2)}) %all-to-all-start.3) | async-done | bytes 2097184 | tf_op jit(solution)/shard_map/all_to_all | solution.py:71
  591.5 3.4 reshape.141
  594.8 2.5 copy.54
  597.3 2.4 copy.51
  (13 shorter events, 0.1 us)
Async XLA Ops:
  7.2 1.6 copy-start.2
  7.2 199.0 %all-gather.3.cloned.1.call-start = ((), (), s32[]{:S(2)}) async-start(), calls=%async_computation.4 | async-start | bytes 10485760 | tf_op jit(solution)/shard_map/all_gather | solution.py:23
  7.9 350.0 %all-gather.5.cloned.1.call-start = ((), (), s32[]{:S(2)}) async-start(), calls=%async_computation.5 | async-start | bytes 10485760 | tf_op jit(solution)/shard_map/all_gather | solution.py:24
  27.3 8.8 %copy-start.4 = (s32[1,32]{1,0:T(1,128)S(1)}, s32[1,32]{1,0:T(1,128)}, u32[]{:S(2)}) copy-start(s32[1,32]{1,0:T(1,128)} %param.13) | copy-start | bytes 388
  27.3 8.9 %copy-start.3 = (f32[1,2,4096]{2,1,0:T(2,128)S(1)}, f32[1,2,4096]{2,1,0:T(2,128)}, u32[]{:S(2)}) copy-start(f32[1,2,4096]{2,1,0:T(2,128)} %param.11) | copy-start | bytes 98308
  30.1 107.3 %all-to-all-start = ((bf16[4,2,131072]{2,1,0:T(2,128)(2,1)}), bf16[4,2,131072]{2,1,0:T(2,128)(2,1)S(1)}, u32[]{:S(2)}, u32[]{:S(2)}) async-start(bf16[4,2,131072]{2,1,0:T(2,128)(2,1)} %reshape.136), calls=%async_computation | async-start | bytes 4194304 | tf_op jit(solution)/shard_map/all_to_all | solution.py:8
  153.1 221.7 %copy-start = (bf16[32,256,128]{2,1,0:T(8,128)(2,1)}, bf16[32,256,128]{2,1,0:T(8,128)(2,1)S(1)}, u32[]{:S(2)}) copy-start(bf16[32,256,128]{2,1,0:T(8,128)(2,1)S(1)} %gather_fusion) | copy-start | bytes 6291460
  392.1 18.1 %all-to-all-start.1 = ((bf16[8,2,32768]{2,1,0:T(2,128)(2,1)}), bf16[8,2,32768]{2,1,0:T(2,128)(2,1)S(1)}, u32[]{:S(2)}, u32[]{:S(2)}) async-start(bf16[8,2,32768]{2,1,0:T(2,128)(2,1)} %reshape.138), calls=%async_computation.1 | async-start | bytes 2097152 | tf_op jit(solution)/shard_map/all_to_all | solution.py:41
  425.0 18.9 %all-to-all-start.2 = ((bf16[32,8,2048]{2,0,1:T(8,128)(2,1)}), bf16[32,8,2048]{2,0,1:T(8,128)(2,1)S(1)}, u32[]{:S(2)}, u32[]{:S(2)}) async-start(bf16[32,8,2048]{2,0,1:T(8,128)(2,1)} %copy.47), calls=%async_computation.2 | async-start | bytes 2097152 | tf_op jit(solution)/shard_map/all_to_all | solution.py:52
  446.2 12.7 %copy-start.1 = (bf16[32,256,128]{2,1,0:T(8,128)(2,1)S(1)}, bf16[32,256,128]{2,1,0:T(8,128)(2,1)}, u32[]{:S(2)}) copy-start(bf16[32,256,128]{2,1,0:T(8,128)(2,1)} %copy-done) | copy-start | bytes 6291460
  539.2 52.3 %all-to-all-start.3 = ((bf16[4,2,131072]{2,1,0:T(2,128)(2,1)}), bf16[4,2,131072]{2,1,0:T(2,128)(2,1)S(1)}, u32[]{:S(2)}, u32[]{:S(2)}) async-start(bf16[4,2,131072]{2,1,0:T(2,128)(2,1)} %reshape.140), calls=%async_computation.3 | async-start | bytes 4194304 | tf_op jit(solution)/shard_map/all_to_all | solution.py:71
Sparse Core Ops, SparseCore 0:
  9.5 196.5 all-gather.2
  207.7 150.1 all-gather.4
where the time goes:
time: 612 us; the launch traced here: 607 us
  waiting for transfers between devices  372 us (61%)
  local copies, waits for them, and re-layouts  89.4 us (15%)
  matrix products  69.9 us (11%)
  other arithmetic  42.7 us (7%)
  starting transfers between devices  18.2 us (3%)
  between operations  14.5 us (2%)
    all_gather x1, waiting for transfers between devices, per_device(): lax.all_gather(cross_up, 'member', axis=3, tiled=True)  152 us
    all_to_all x1, waiting for transfers between devices, per_device(): lax.all_to_all(slabs, 'member', split_axis=1, concat_axis=2, tiled=True)  101 us
    all_gather x1, waiting for transfers between devices, per_device(): lax.all_gather(cross_down, 'member', axis=3, tiled=True)  53.1 us
    all_to_all x1, waiting for transfers between devices, per_device(): lax.all_to_all(unplaced, 'member', split_axis=2, concat_axis=1, tiled=True)  45.3 us
    unnamed x3, other arithmetic  35.8 us
    unnamed x23, local copies, waits for them, and re-layouts  33.3 us
    reshape x2, local copies, waits for them, and re-layouts, per_device(): total.reshape(row_count, features, slot_width)[:, inverse_place]  27.4 us
    dot_general x2, matrix products, per_device(): jnp.dot(dhidden, whole_down[0, depth].T, preferred_element_type=jnp.float32)  23.7 us
  transfers between devices with their start and end apart: 6, of which 6 were waited for; matrix products, arithmetic and copies ran while one was open for 8% of the time, Pallas kernels for 0%

commit v1 on v0

--- a/solution.py
+++ b/solution.py
@@ -68,7 +68,12 @@
     unplaced = total.reshape(row_count, features, slot_width)[:, inverse_place].reshape(
         1, row_count, full_width
     )
-    slab_grad = lax.all_to_all(unplaced, "member", split_axis=2, concat_axis=1, tiled=True)
+    slab_grad = jnp.concatenate(
+        lax.all_to_all(
+            jnp.stack(jnp.split(unplaced, lax.axis_size("member"), axis=2)), "member", 0, 0
+        ),
+        axis=1,
+    )
     return (interactions, slab_grad)
 
 

time: 612 us -> 571 us (0.933)
  other arithmetic: 42.7 us -> 21.5 us
  local copies, waits for them, and re-layouts: 89.4 us -> 68.6 us
    reshape x2 -> x1, local copies, waits for them, and re-layouts: 27.4 us -> 2.16 us  [per_device(): total.reshape(row_count, features, slot_width)[:, inverse_place]]
    unnamed x3 -> x2, other arithmetic: 35.8 us -> 12.9 us
    unnamed x23 -> x22, local copies, waits for them, and re-layouts: 33.3 us -> 37.6 us
where the time goes in v1:
time: 571 us; the launch traced here: 566 us
  waiting for transfers between devices  374 us (65%)
  matrix products  69.9 us (12%)
  local copies, waits for them, and re-layouts  68.6 us (12%)
  other arithmetic  21.5 us (4%)
  starting transfers between devices  18.1 us (3%)
  between operations  14.3 us (3%)
    all_gather x1, waiting for transfers between devices, per_device(): lax.all_gather(cross_up, 'member', axis=3, tiled=True)  152 us
    all_to_all x1, waiting for transfers between devices, per_device(): lax.all_to_all(slabs, 'member', split_axis=1, concat_axis=2, tiled=True)  101 us
    all_gather x1, waiting for transfers between devices, per_device(): lax.all_gather(cross_down, 'member', axis=3, tiled=True)  53.1 us
    all_to_all x1, waiting for transfers between devices, per_device(): lax.all_to_all(jnp.stack(jnp.split(unplaced, lax.axis_size('member'), axi...  45.3 us
    unnamed x22, local copies, waits for them, and re-layouts  37.6 us
    dot_general x2, matrix products, per_device(): jnp.dot(dhidden, whole_down[0, depth].T, preferred_element_type=jnp.float32)  23.7 us
    dot_general x2, matrix products, per_device(): jnp.dot(hidden, whole_up[0, depth].T, preferred_element_type=jnp.float32)  16.9 us
    unnamed x2, other arithmetic  12.9 us
  transfers between devices with their start and end apart: 6, of which 6 were waited for; matrix products, arithmetic and copies ran while one was open for 8% of the time, Pallas kernels for 0%

profile of v1, /device:TPU:2, one launch (start us, length us, event | category | flops | bytes accessed | tf_op | source)
XLA Modules:
  0.0 565.8 jit_solution(3872242795952572050)
XLA Ops:
  7.2 0.0 copy-start.2
  7.2 0.0 all-gather.3.cloned.1.call-start
  7.2 0.7 all-gather.3.cloned.1.call-update
  7.9 0.0 all-gather.5.cloned.1.call-start
  8.0 0.7 all-gather.5.cloned.1.call-update
  8.7 0.1 copy-done.2
  8.8 5.2 copy.101
  13.9 0.5 broadcast.88
  14.5 12.8 %reduce = bf16[1024,1024]{1,0:T(8,128)(2,1)S(1)} reduce(bf16[1024,1,1024]{2,1,0:T(2,128)(2,1)} %bitcast.162, bf16[]{:T(256)} %broadcast.88), dimensions={1}, to_apply=%bitcast.158.reduce_sub_computation | reduce | bytes 4194306
  27.2 0.0 copy-start.5
  27.2 0.0 copy-start.4
  27.3 2.8 reshape.140
  30.0 5.2 all-to-all-start
  35.2 0.7 compare_select_fusion
  35.9 0.0 copy-done.5
  36.0 0.0 copy-done.4
  36.0 101.4 %all-to-all-done = bf16[4,2,131072]{2,1,0:T(2,128)(2,1)S(1)} async-done(((bf16[4,2,131072]{2,1,0:T(2,128)(2,1)}), bf16[4,2,131072]{2,1,0:T(2,128)(2,1)S(1)}, u32[]{:S(2)}, u32[]{:S(2)}) %all-to-all-start) | async-done | bytes 2097184 | tf_op jit(solution)/shard_map/all_to_all | solution.py:8
  137.4 3.3 reshape.141
  140.8 3.1 copy.64
  143.8 2.6 copy.54
  146.4 4.1 copy.55
  150.5 2.5 gather_fusion
  153.0 0.0 copy-start
  153.1 53.1 %all-gather.3.cloned.1.call-done = bf16[1,2,4096,512]{3,2,1,0:T(8,128)(2,1)} async-done(((bf16[1,2,4096,128]{3,2,1,0:T(8,128)(2,1)}), bf16[1,2,4096,512]{3,2,1,0:T(8,128)(2,1)}) %all-gather.3.cloned.1.call-update) | async-done | bytes 8388624 | tf_op jit(solution)/shard_map/all_gather | solution.py:23
  206.2 151.8 %all-gather.5.cloned.1.call-done = bf16[1,2,4096,512]{3,2,1,0:T(8,128)(2,1)} async-done(((bf16[1,2,4096,128]{3,2,1,0:T(8,128)(2,1)}), bf16[1,2,4096,512]{3,2,1,0:T(8,128)(2,1)}) %all-gather.5.cloned.1.call-update) | async-done | bytes 8388624 | tf_op jit(solution)/shard_map/all_gather | solution.py:24
  357.9 7.8 %convolution_add_fusion.3 = f32[256,4096]{1,0:T(8,128)} fusion(bf16[1,2,4096,512]{3,2,1,0:T(8,128)(2,1)} %all-gather.5.cloned.1.call-done, f32[4096]{0:T(1024)S(1)} %bitcast.175, bf16[1,2,4096,512]{3,2,1,0:T(8,128)(2,1)} %all-gather.3.cloned.1.call-done, bf16[32,256,128]{2,1,0:T(8,128)(2,1)S(1)} %gather_fusion), kind=kOutput, calls=%fused_computation.16 | convolution fusion | flops 2148663296 | bytes 14696448 | tf_op jit(solution)/shard_map/dot_general | solution.py:33
  365.7 9.1 %convolution_add_fusion.2 = f32[256,4096]{1,0:T(8,128)} fusion(bf16[1,2,4096,512]{3,2,1,0:T(8,128)(2,1)} %all-gather.5.cloned.1.call-done, f32[4096]{0:T(1024)S(1)} %bitcast.174, bf16[1,2,4096,512]{3,2,1,0:T(8,128)(2,1)} %all-gather.3.cloned.1.call-done, f32[256,4096]{1,0:T(8,128)} %convolution_add_fusion.3, bf16[32,256,128]{2,1,0:T(8,128)(2,1)S(1)} %gather_fusion), kind=kOutput, calls=%fused_computation.15 | convolution fusion | flops 2152857600 | bytes 18890752 | tf_op jit(solution)/shard_map/dot_general | solution.py:33
  374.8 12.7 %fusion.15 = bf16[256,2048]{1,0:T(8,128)(2,1)S(1)} fusion(bf16[1,4096,2048]{2,1,0:T(8,128)(2,1)} %param.12, f32[256,4096]{1,0:T(8,128)} %convolution_add_fusion.2, f32[256,4096]{1,0:T(8,128)} %convolution_add_fusion.3, bf16[32,256,128]{2,1,0:T(8,128)(2,1)S(1)} %gather_fusion), kind=kOutput, calls=%fused_computation.32 | convolution fusion | flops 4303880192 | bytes 28311552 | tf_op jit(solution)/shard_map/dot_general | solution.py:38
  387.5 1.4 gather_fusion.1
  388.9 0.0 copy-start.3
  388.9 1.5 reduce.1
  390.4 14.1 %reshape.142 = bf16[8,2,32768]{2,1,0:T(2,128)(2,1)} reshape(bf16[256,2048]{1,0:T(8,128)(2,1)S(1)} %reduce.1) | data formatting | bytes 2097152
  404.5 4.2 all-to-all-start.1
  408.7 0.0 copy-done.3
  408.7 0.1 convert_bitcast_fusion
  408.8 0.4 copy.69
  409.2 1.8 copy.59
  411.0 11.5 %all-to-all-done.1 = bf16[8,2,32768]{2,1,0:T(2,128)(2,1)S(1)} async-done(((bf16[8,2,32768]{2,1,0:T(2,128)(2,1)}), bf16[8,2,32768]{2,1,0:T(2,128)(2,1)S(1)}, u32[]{:S(2)}, u32[]{:S(2)}) %all-to-all-start.1) | async-done | bytes 1048608 | tf_op jit(solution)/shard_map/all_to_all | solution.py:41
  422.6 3.4 reshape.143
  426.0 2.2 copy.65
  428.2 1.5 copy.58
  429.7 1.6 reshape.95
  431.3 3.0 multiply_convert_fusion
  434.3 1.5 reshape.99
  435.8 1.5 copy.60
  437.4 5.0 all-to-all-start.2
  442.4 3.2 sort.34
  445.5 1.6 sort.35
  447.2 9.1 %all-to-all-done.2 = bf16[32,8,2048]{2,0,1:T(8,128)(2,1)S(1)} async-done(((bf16[32,8,2048]{2,0,1:T(8,128)(2,1)}), bf16[32,8,2048]{2,0,1:T(8,128)(2,1)S(1)}, u32[]{:S(2)}, u32[]{:S(2)}) %all-to-all-start.2) | async-done | bytes 1048608 | tf_op jit(solution)/shard_map/all_to_all | solution.py:52
  456.3 2.3 gather_fusion.2
  458.6 12.7 %fusion = f32[256,4096]{1,0:T(8,128)} fusion(bf16[256,2048]{1,0:T(8,128)(2,1)} %gather_fusion.2, bf16[1,4096,2048]{2,1,0:T(8,128)(2,1)} %param.12), kind=kOutput, calls=%fused_computation.4 | convolution fusion | flops 4294967296 | bytes 22020096 | tf_op jit(solution)/shard_map/dot_general | solution.py:55
  471.3 0.0 copy-done.1
  471.3 10.2 %convolution_add_fusion.1 = f32[256,4096]{1,0:T(8,128)} fusion(f32[256,4096]{1,0:T(8,128)} %fusion, bf16[1,2,4096,512]{3,2,1,0:T(8,128)(2,1)} %all-gather.3.cloned.1.call-done, bf16[1,2,4096,512]{3,2,1,0:T(8,128)(2,1)} %all-gather.5.cloned.1.call-done, bf16[32,256,128]{2,1,0:T(8,128)(2,1)S(1)} %copy-done.1), kind=kOutput, calls=%fused_computation.14 | convolution fusion | flops 2151809024 | bytes 23068672 | tf_op jit(solution)/shard_map/dot_general | solution.py:63
  481.6 13.5 %fusion.26 = bf16[32,32,8,128]{3,2,1,0:T(8,128)(2,1)} fusion(f32[256,4096]{1,0:T(8,128)} %convolution_add_fusion.1, f32[256,4096]{1,0:T(8,128)} %convolution_add_fusion.3, f32[256,4096]{1,0:T(8,128)} %fusion, f32[256,4096]{1,0:T(8,128)} %convolution_add_fusion.2, bf16[1,2,4096,512]{3,2,1,0:T(8,128)(2,1)} %all-gather.3.cloned.1.call-done, ...), kind=kOutput, calls=%fused_computation.44 | convolution fusion | flops 2157051904 | bytes 33554432 | tf_op jit(solution)/shard_map/dot_general | solution.py:63
  495.0 2.2 copy.100
  497.2 2.1 gather_fusion.3
  499.3 3.3 copy.62
  502.6 0.1 slice_bitcast_fusion.33
  502.7 1.6 pad_maximum_fusion
  504.3 3.6 all-to-all-start.3
  507.9 0.8 convolution_multiply_fusion
  508.8 2.5 copy.99
  511.3 45.3 %all-to-all-done.3 = bf16[4,1,256,1024]{2,3,1,0:T(8,128)(2,1)S(1)} async-done(((bf16[4,1,256,1024]{2,3,1,0:T(8,128)(2,1)}), bf16[4,1,256,1024]{2,3,1,0:T(8,128)(2,1)S(1)}, u32[]{:S(2)}, u32[]{:S(2)}) %all-to-all-start.3) | async-done | bytes 2097184 | tf_op jit(solution)/shard_map/all_to_all | solution.py:72
  556.6 2.4 copy.63
  (12 shorter events, 0.1 us)
Async XLA Ops:
  7.2 1.6 copy-start.2
  7.2 199.0 %all-gather.3.cloned.1.call-start = ((), (), s32[]{:S(2)}) async-start(), calls=%async_computation.4 | async-start | bytes 10485760 | tf_op jit(solution)/shard_map/all_gather | solution.py:23
  7.9 350.0 %all-gather.5.cloned.1.call-start = ((), (), s32[]{:S(2)}) async-start(), calls=%async_computation.5 | async-start | bytes 10485760 | tf_op jit(solution)/shard_map/all_gather | solution.py:24
  27.2 8.7 %copy-start.5 = (s32[1,32]{1,0:T(1,128)S(1)}, s32[1,32]{1,0:T(1,128)}, u32[]{:S(2)}) copy-start(s32[1,32]{1,0:T(1,128)} %param.13) | copy-start | bytes 388
  27.2 8.7 %copy-start.4 = (f32[1,2,4096]{2,1,0:T(2,128)S(1)}, f32[1,2,4096]{2,1,0:T(2,128)}, u32[]{:S(2)}) copy-start(f32[1,2,4096]{2,1,0:T(2,128)} %param.11) | copy-start | bytes 98308
  30.0 107.4 %all-to-all-start = ((bf16[4,2,131072]{2,1,0:T(2,128)(2,1)}), bf16[4,2,131072]{2,1,0:T(2,128)(2,1)S(1)}, u32[]{:S(2)}, u32[]{:S(2)}) async-start(bf16[4,2,131072]{2,1,0:T(2,128)(2,1)} %reshape.140), calls=%async_computation | async-start | bytes 4194304 | tf_op jit(solution)/shard_map/all_to_all | solution.py:8
  153.0 221.7 %copy-start = (bf16[32,256,128]{2,1,0:T(8,128)(2,1)}, bf16[32,256,128]{2,1,0:T(8,128)(2,1)S(1)}, u32[]{:S(2)}) copy-start(bf16[32,256,128]{2,1,0:T(8,128)(2,1)S(1)} %gather_fusion) | copy-start | bytes 6291460
  388.9 19.8 %copy-start.3 = (bf16[32,16384]{1,0:T(8,128)(2,1)S(1)}, bf16[32,16384]{1,0:T(8,128)(2,1)}, u32[]{:S(2)}) copy-start(bf16[32,16384]{1,0:T(8,128)(2,1)} %param.15) | copy-start | bytes 3145732
  404.5 18.1 %all-to-all-start.1 = ((bf16[8,2,32768]{2,1,0:T(2,128)(2,1)}), bf16[8,2,32768]{2,1,0:T(2,128)(2,1)S(1)}, u32[]{:S(2)}, u32[]{:S(2)}) async-start(bf16[8,2,32768]{2,1,0:T(2,128)(2,1)} %reshape.142), calls=%async_computation.1 | async-start | bytes 2097152 | tf_op jit(solution)/shard_map/all_to_all | solution.py:41
  437.4 18.9 %all-to-all-start.2 = ((bf16[32,8,2048]{2,0,1:T(8,128)(2,1)}), bf16[32,8,2048]{2,0,1:T(8,128)(2,1)S(1)}, u32[]{:S(2)}, u32[]{:S(2)}) async-start(bf16[32,8,2048]{2,0,1:T(8,128)(2,1)} %copy.60), calls=%async_computation.2 | async-start | bytes 2097152 | tf_op jit(solution)/shard_map/all_to_all | solution.py:52
  458.6 12.7 %copy-start.1 = (bf16[32,256,128]{2,1,0:T(8,128)(2,1)S(1)}, bf16[32,256,128]{2,1,0:T(8,128)(2,1)}, u32[]{:S(2)}) copy-start(bf16[32,256,128]{2,1,0:T(8,128)(2,1)} %copy-done) | copy-start | bytes 6291460
  504.3 52.3 %all-to-all-start.3 = ((bf16[4,1,256,1024]{2,3,1,0:T(8,128)(2,1)}), bf16[4,1,256,1024]{2,3,1,0:T(8,128)(2,1)S(1)}, u32[]{:S(2)}, u32[]{:S(2)}) async-start(bf16[4,1,256,1024]{2,3,1,0:T(8,128)(2,1)} %pad_maximum_fusion), calls=%async_computation.3 | async-start | bytes 4194304 | tf_op jit(solution)/shard_map/all_to_all | solution.py:72
Sparse Core Ops, SparseCore 0:
  9.5 196.5 all-gather.2
  207.7 150.1 all-gather.4
